TPU v7x, 32 devices: a whole 2x2x4 slice. The times are simulated.
32 devices in a mesh: comp: 4 (over y, x), dom: 8 (over z, core).
Axes of the slice: x: 2, y: 2, z: 4, core: 2. Of those that a mesh axis runs over, the one named last changes fastest.
Arguments:
- atm_fields: bfloat16 [24, 65536], P(None, ('comp', 'dom')), may hold values from -6 to 6
- send_cols: int32 [4, 8, 4, 4, 256], P('comp', 'dom'), may hold values from 0 to 2047
- live_blocks: int32 [4, 8, 4], P('comp', 'dom'), may hold values from 1 to 4, as said below
- remap_weights: bfloat16 [4, 8, 4, 4, 256, 256], P('comp', 'dom'), may hold values from -0.375 to 0.375
- row_map: int32 [4, 8, 4, 4, 256], P('comp', 'dom'), may hold values from 0 to 4095
- ocean_depth: float32 [256, 512], P('dom', 'comp'), may hold values from 0.25 to 8
- wet_mask: int32 [256, 512], P('dom', 'comp'), may hold values 0 or 1
- sea_level: float32 [256, 512], P('dom', 'comp'), may hold values from -3 to 3
- east_vel: float32 [256, 512], P('dom', 'comp'), may hold values from -0.3 to 0.3
- north_vel: float32 [256, 512], P('dom', 'comp'), may hold values from -0.3 to 0.3
Outputs:
- ocean_fluxes: float32 [24, 256, 512], P(None, 'dom', 'comp')
- ocean_state: float32 [3, 256, 512], P(None, 'dom', 'comp')
Inputs may be any that keep to these rules, and one draw needn't show every extreme that they name: `live_blocks`: every receiving device has exactly 4 live blocks from at least one source group.
All inputs are finite; a program needn't handle non-finite values. No bound on the sum of `wet_mask` on one device may be relied on, other than what follows from the above.
Results may differ from a plain program's by a relative error of at most 0.0003.
Values may be sent and summed in bfloat16 or wider, within the bound.
A program may use at most 64 MiB of HBM per device.

v0:
```python
import jax
import jax.numpy as jnp
from jax import lax
from jax.sharding import PartitionSpec as P

NSUB = 4


courant = 0.5
friction = 0.05


def padded(cells, sides, width):
    for axis, dim in sides:
        count = lax.axis_size(axis)
        ends = count - 1
        head = lax.slice_in_dim(cells, 0, width, axis=dim)
        tail = lax.slice_in_dim(cells, cells.shape[dim] - width, cells.shape[dim], axis=dim)
        cells = jnp.concatenate(
            [
                lax.ppermute(tail, axis, [(i, (i + 1) % count) for i in range(ends)]),
                cells,
                lax.ppermute(head, axis, [((i + 1) % count, i) for i in range(ends)]),
            ],
            axis=dim,
        )
    return cells


def level_update(level, flux_x, flux_y, fresh, wetness, step_dt):
    diverge = 0.5 * (flux_x[1:-1, 2:] - flux_x[1:-1, :-2] + (flux_y[2:, 1:-1] - flux_y[:-2, 1:-1]))
    return wetness[1:-1, 1:-1] * (level[1:-1, 1:-1] + step_dt * (fresh[1:-1, 1:-1] - diverge))


def velocity_update(east, north, level_ext, rotation, push_x, push_y, wetness, step_dt):
    grad_x = 0.5 * (level_ext[1:-1, 2:] - level_ext[1:-1, :-2])
    grad_y = 0.5 * (level_ext[2:, 1:-1] - level_ext[:-2, 1:-1])
    new_east = wetness * (east + step_dt * (rotation * north - grad_x + push_x - friction * east))
    new_north = wetness * (
        north + step_dt * (-rotation * east - grad_y + push_y - friction * north)
    )
    return (new_east, new_north)


def deposit(total, blocks, weights, alive, targets):
    contrib = jnp.einsum("sknb,skob->skno", blocks, weights, preferred_element_type=jnp.float32)
    contrib = contrib * alive[:, :, None, None]
    flat = jnp.transpose(contrib, (2, 0, 1, 3)).reshape(total.shape[0], -1)
    return total.at[:, targets.reshape(-1)].add(flat)


def shards(
    atm_fields,
    send_cols,
    live_blocks,
    remap_weights,
    row_map,
    ocean_depth,
    wet_mask,
    sea_level,
    east_vel,
    north_vel,
):
    weights = remap_weights[0, 0]
    targets = row_map[0, 0]
    live = live_blocks[0, 0]
    capacity = weights.shape[1]
    nfield = atm_fields.shape[0]
    width = atm_fields.shape[1]
    nrows_dev, ncols_dev = ocean_depth.shape
    slots = jnp.arange(capacity, dtype=jnp.int32)
    alive = (slots[None, :] < live[:, None]).astype(jnp.float32)
    wetness = wet_mask.astype(jnp.float32)
    empty = jnp.zeros((nfield, nrows_dev * ncols_dev), jnp.float32)
    lists = lax.all_to_all(send_cols[0, 0], "comp", split_axis=0, concat_axis=0, tiled=True)
    total = empty
    piece = lax.all_gather(atm_fields, "comp", axis=1, tiled=True)
    start = jnp.int32(0)
    for shard_idx in range(piece.shape[1] // width):
        source = start // width + shard_idx
        section = piece[:, shard_idx * width : (shard_idx + 1) * width]
        columns = lax.dynamic_index_in_dim(lists, source, 0, keepdims=True)
        picked = jnp.take(section, columns.reshape(-1), axis=1).reshape(nfield, 1, capacity, -1)
        picked = jnp.transpose(picked, (1, 2, 0, 3))
        total = deposit(
            total,
            picked,
            lax.dynamic_index_in_dim(weights, source, 0, keepdims=True),
            lax.dynamic_index_in_dim(alive, source, 0, keepdims=True),
            lax.dynamic_index_in_dim(targets, source, 0, keepdims=True),
        )
    fluxes = total
    fluxes = fluxes.reshape(nfield, nrows_dev, ncols_dev)
    push_x = fluxes[0] / ocean_depth
    push_y = fluxes[1] / ocean_depth
    fresh = fluxes[2]
    statics = jnp.stack([ocean_depth, wetness, fresh])
    statics_ext = padded(statics, (("comp", 2), ("dom", 1)), 2)
    total_rows = nrows_dev * lax.axis_size("dom")
    global_rows = lax.axis_index("dom") * nrows_dev + jnp.arange(nrows_dev, dtype=jnp.int32)
    rotation = (0.1 + 0.4 * (global_rows.astype(jnp.float32) + 0.5) / total_rows)[:, None]
    root_depth = jnp.sqrt(ocean_depth)
    level, east, north = (sea_level, east_vel, north_vel)
    for substep in range(NSUB):
        local_speed = jnp.max(root_depth + wetness * (jnp.abs(east) + jnp.abs(north)))
        fastest = lax.pmax(local_speed, ("comp", "dom"))
        step_dt = courant / fastest
        state = jnp.stack([level, east, north])
        state_ext = padded(state, (("comp", 2), ("dom", 1)), 2)
        depth_ext, wet_ext, fresh_ext = (statics_ext[0], statics_ext[1], statics_ext[2])
        flux_x = depth_ext * state_ext[1] * wet_ext
        flux_y = depth_ext * state_ext[2] * wet_ext
        level_ext = level_update(state_ext[0], flux_x, flux_y, fresh_ext, wet_ext, step_dt)
        new_level = level_ext[1:-1, 1:-1]
        east, north = velocity_update(
            east, north, level_ext, rotation, push_x, push_y, wetness, step_dt
        )
        level = new_level
    return (fluxes, jnp.stack([level, east, north]))


def solution(mesh):
    in_specs = (
        P(None, ("comp", "dom")),
        P("comp", "dom", None, None, None),
        P("comp", "dom", None),
        P("comp", "dom", None, None, None, None),
        P("comp", "dom", None, None, None),
        P("dom", "comp"),
        P("dom", "comp"),
        P("dom", "comp"),
        P("dom", "comp"),
        P("dom", "comp"),
    )
    out_specs = (P(None, "dom", "comp"), P(None, "dom", "comp"))
    return jax.shard_map(shards, mesh=mesh, in_specs=in_specs, out_specs=out_specs, check_vma=False)
```

profile of v0, /device:TPU:0, one launch (start us, length us, event | category | flops | bytes accessed | tf_op | source)
XLA Modules:
  0.0 339.7 jit_solution(9952452214590874664)
XLA Ops:
  0.6 5.2 %all-to-all-start = ((s32[4,4,256]{2,1,0:T(4,128)}), s32[4,4,256]{2,1,0:T(4,128)S(1)}, u32[]{:S(2)}, u32[]{:S(2)}) async-start(s32[4,4,256]{2,1,0:T(4,128)} %bitcast.279), calls=%async_computation | async-start | bytes 32768 | tf_op jit(solution)/shard_map/all_to_all | solution.py:75
  6.7 3.9 %collective-permute-start.4 = (f32[3,32,2]{2,1,0:T(8,128)S(1)}, f32[3,32,2]{2,1,0:T(8,128)S(1)}, u32[]{:S(2)}, u32[]{:S(2)}) collective-permute-start(f32[3,32,2]{2,1,0:T(8,128)S(1)} %get-tuple-element.55), channel_id=1, source_target_pairs={{0,8},{8,16},{16,24},{1,9},{9,17},{17,25},{2,10},{10,18},{18,26},{... | collective-permute-start | bytes 2312 | tf_op jit(solution)/shard_map/ppermute | solution.py:21
  10.6 1.3 collective-permute-start.5
  13.1 21.7 %all_gather.3 = bf16[24,8192]{0,1:T(8,128)(2,1)S(1)} all-gather(bf16[24,2048]{0,1:T(8,128)(2,1)S(1)} %copy.18), channel_id=1, replica_groups=mesh['comp'=4,'dom'=8] {'comp'}, dimensions={1}, use_global_device_ids=true | all-gather | bytes 491520 | tf_op jit(solution)/shard_map/all_gather | solution.py:77
  40.4 39.7 %pmax.28 = f32[]{:T(128)} all-reduce(f32[]{:T(128)} %add_reduce_fusion.3), channel_id=1, replica_groups=mesh['comp'=4,'dom'=8] {'comp','dom'}, use_global_device_ids=true, to_apply=%region_5.7 | all-reduce | flops 1 | bytes 8 | tf_op jit(solution)/shard_map/pmax | solution.py:106
  81.5 1.9 collective-permute-start.6
  88.3 5.2 %gather_fusion = bf16[1024,24]{1,0:T(8,128)(2,1)} fusion(bf16[24,2048]{0,1:T(8,128)(2,1)} %get-tuple-element.24, s32[1024]{0:T(1024)S(1)} %fusion.116), kind=kCustom, calls=%fused_computation.clone | custom fusion | bytes 102400 | tf_op jit(solution)/shard_map/jit(_take)/gather | solution.py:83
  96.7 5.5 %gather_fusion.1 = bf16[1024,24]{1,0:T(8,128)(2,1)} fusion(bf16[24,2048]{0,1:T(8,128)(2,1)} %get-tuple-element.23, s32[1024]{0:T(1024)} %fusion.117), kind=kCustom, calls=%fused_computation.1.clone | custom fusion | bytes 102400 | tf_op jit(solution)/shard_map/jit(_take)/gather | solution.py:83
  105.6 3.8 %gather_fusion.2 = bf16[1024,24]{1,0:T(8,128)(2,1)S(1)} fusion(bf16[24,2048]{0,1:T(8,128)(2,1)S(1)} %get-tuple-element.22, s32[1024]{0:T(1024)} %fusion.118), kind=kCustom, calls=%fused_computation.2.clone | custom fusion | bytes 102400 | tf_op jit(solution)/shard_map/jit(_take)/gather | solution.py:83
  110.9 3.2 gather_fusion.3
  115.0 6.9 %scatter_custom_fusion = f32[24,4096]{0,1:T(8,128)S(1)} fusion(s32[1024]{0:T(1024)} %bitcast.284, f32[1024,24]{1,0:T(8,128)} %copy.21, f32[]{:T(128)} %constant.116.clone.1), kind=kCustom, calls=%fused_computation.19 | custom fusion | flops 24576 | bytes 393728 | tf_op jit(solution)/shard_map/scatter-add | solution.py:49
  122.0 7.2 %scatter_fusion = f32[24,4096]{0,1:T(8,128)S(1)} fusion(f32[24,4096]{0,1:T(8,128)S(1)} %scatter_custom_fusion, s32[1024]{0:T(1024)S(1)} %bitcast.276, f32[1024,24]{1,0:T(8,128)} %copy.24), kind=kCustom, calls=%fused_computation.5 | custom fusion | flops 24576 | bytes 299008 | tf_op jit(solution)/shard_map/scatter-add | solution.py:49
  129.2 6.8 %scatter_fusion.1 = f32[24,4096]{0,1:T(8,128)S(1)} fusion(f32[24,4096]{0,1:T(8,128)S(1)} %scatter_fusion, s32[1024]{0:T(1024)S(1)} %bitcast.277, f32[1024,24]{1,0:T(8,128)S(1)} %copy.27), kind=kCustom, calls=%fused_computation.6 | custom fusion | flops 24576 | bytes 299008 | tf_op jit(solution)/shard_map/scatter-add | solution.py:49
  136.0 7.0 %scatter_fusion.2 = f32[24,4096]{0,1:T(8,128)S(1)} fusion(f32[24,4096]{0,1:T(8,128)S(1)} %scatter_fusion.1, s32[1024]{0:T(1024)S(1)} %bitcast.278, f32[1024,24]{1,0:T(8,128)S(1)} %copy.30), kind=kCustom, calls=%fused_computation.7 | custom fusion | flops 24576 | bytes 299008 | tf_op jit(solution)/shard_map/scatter-add | solution.py:49
  143.0 2.8 slice_reduce_fusion.1
  145.9 4.2 %collective-permute-start = (f32[3,32,2]{2,1,0:T(8,128)S(1)}, f32[3,32,2]{2,1,0:T(8,128)S(1)}, u32[]{:S(2)}, u32[]{:S(2)}) collective-permute-start(f32[3,32,2]{2,1,0:T(8,128)S(1)} %get-tuple-element.53), channel_id=1, source_target_pairs={{0,8},{8,16},{16,24},{1,9},{9,17},{17,25},{2,10},{10,18},{18,26},{... | collective-permute-start | bytes 2312 | tf_op jit(solution)/shard_map/ppermute | solution.py:21
  150.1 1.3 collective-permute-start.1
  152.3 3.8 %collective-permute-done.1 = f32[3,32,2]{2,1,0:T(8,128)S(1)} collective-permute-done((f32[3,32,2]{2,1,0:T(8,128)S(1)}, f32[3,32,2]{2,1,0:T(8,128)S(1)}, u32[]{:S(2)}, u32[]{:S(2)}) %collective-permute-start.1) | collective-permute-done | bytes 800 | tf_op jit(solution)/shard_map/ppermute | solution.py:23
  156.2 2.8 collective-permute-start.2
  160.3 4.4 %collective-permute-done.3 = f32[3,2,132]{2,1,0:T(2,128)S(1)} collective-permute-done((f32[3,2,132]{2,1,0:T(2,128)S(1)}, f32[3,2,132]{2,1,0:T(2,128)S(1)}, u32[]{:S(2)}, u32[]{:S(2)}) %collective-permute-start.3) | collective-permute-done | bytes 3200 | tf_op jit(solution)/shard_map/ppermute | solution.py:23
  165.8 4.5 %collective-permute-start.8 = (f32[3,32,2]{2,1,0:T(8,128)S(1)}, f32[3,32,2]{2,1,0:T(8,128)S(1)}, u32[]{:S(2)}, u32[]{:S(2)}) collective-permute-start(f32[3,32,2]{2,1,0:T(8,128)S(1)} %get-tuple-element.51), channel_id=1, source_target_pairs={{0,8},{8,16},{16,24},{1,9},{9,17},{17,25},{2,10},{10,18},{18,26},{... | collective-permute-start | bytes 2312 | tf_op jit(solution)/shard_map/ppermute | solution.py:21
  172.0 4.3 %collective-permute-done.9 = f32[3,32,2]{2,1,0:T(8,128)S(1)} collective-permute-done((f32[3,32,2]{2,1,0:T(8,128)S(1)}, f32[3,32,2]{2,1,0:T(8,128)S(1)}, u32[]{:S(2)}, u32[]{:S(2)}) %collective-permute-start.9) | collective-permute-done | bytes 800 | tf_op jit(solution)/shard_map/ppermute | solution.py:23
  176.4 2.9 collective-permute-start.10
  180.5 41.9 %pmax.29 = f32[]{:T(128)} all-reduce(f32[]{:T(128)} %get-tuple-element.16), channel_id=1, replica_groups=mesh['comp'=4,'dom'=8] {'comp','dom'}, use_global_device_ids=true, to_apply=%region_7.9 | all-reduce | flops 1 | bytes 8 | tf_op jit(solution)/shard_map/pmax | solution.py:106
  224.3 4.2 %collective-permute-start.12 = (f32[3,32,2]{2,1,0:T(8,128)S(1)}, f32[3,32,2]{2,1,0:T(8,128)S(1)}, u32[]{:S(2)}, u32[]{:S(2)}) collective-permute-start(f32[3,32,2]{2,1,0:T(8,128)S(1)} %get-tuple-element.49), channel_id=1, source_target_pairs={{0,8},{8,16},{16,24},{1,9},{9,17},{17,25},{2,10},{10,18},{18,26},{... | collective-permute-start | bytes 2312 | tf_op jit(solution)/shard_map/ppermute | solution.py:21
  228.5 1.3 collective-permute-start.13
  230.2 4.3 %collective-permute-done.13 = f32[3,32,2]{2,1,0:T(8,128)S(1)} collective-permute-done((f32[3,32,2]{2,1,0:T(8,128)S(1)}, f32[3,32,2]{2,1,0:T(8,128)S(1)}, u32[]{:S(2)}, u32[]{:S(2)}) %collective-permute-start.13) | collective-permute-done | bytes 800 | tf_op jit(solution)/shard_map/ppermute | solution.py:23
  237.1 41.7 %pmax.30 = f32[]{:T(128)} all-reduce(f32[]{:T(128)} %get-tuple-element.13), channel_id=1, replica_groups=mesh['comp'=4,'dom'=8] {'comp','dom'}, use_global_device_ids=true, to_apply=%region_9.11 | all-reduce | flops 1 | bytes 8 | tf_op jit(solution)/shard_map/pmax | solution.py:106
  280.6 4.2 %collective-permute-start.16 = (f32[3,32,2]{2,1,0:T(8,128)S(1)}, f32[3,32,2]{2,1,0:T(8,128)S(1)}, u32[]{:S(2)}, u32[]{:S(2)}) collective-permute-start(f32[3,32,2]{2,1,0:T(8,128)S(1)} %get-tuple-element.47), channel_id=1, source_target_pairs={{0,8},{8,16},{16,24},{1,9},{9,17},{17,25},{2,10},{10,18},{18,26},{... | collective-permute-start | bytes 2312 | tf_op jit(solution)/shard_map/ppermute | solution.py:21
  286.5 4.3 %collective-permute-done.17 = f32[3,32,2]{2,1,0:T(8,128)S(1)} collective-permute-done((f32[3,32,2]{2,1,0:T(8,128)S(1)}, f32[3,32,2]{2,1,0:T(8,128)S(1)}, u32[]{:S(2)}, u32[]{:S(2)}) %collective-permute-start.17) | collective-permute-done | bytes 800 | tf_op jit(solution)/shard_map/ppermute | solution.py:23
  293.5 1.4 copy.31
  294.8 43.1 %pmax.31 = f32[]{:T(128)} all-reduce(f32[]{:T(128)} %get-tuple-element.10), channel_id=1, replica_groups=mesh['comp'=4,'dom'=8] {'comp','dom'}, use_global_device_ids=true, to_apply=%region_11.13 | all-reduce | flops 1 | bytes 8 | tf_op jit(solution)/shard_map/pmax | solution.py:106
  (158 shorter events, 39.0 us)
Async XLA Ops:
  0.6 84.0 %all-to-all-start = ((s32[4,4,256]{2,1,0:T(4,128)}), s32[4,4,256]{2,1,0:T(4,128)S(1)}, u32[]{:S(2)}, u32[]{:S(2)}) async-start(s32[4,4,256]{2,1,0:T(4,128)} %bitcast.279), calls=%async_computation | async-start | bytes 32768 | tf_op jit(solution)/shard_map/all_to_all | solution.py:75
  6.7 74.1 %collective-permute-start.4 = (f32[3,32,2]{2,1,0:T(8,128)S(1)}, f32[3,32,2]{2,1,0:T(8,128)S(1)}, u32[]{:S(2)}, u32[]{:S(2)}) collective-permute-start(f32[3,32,2]{2,1,0:T(8,128)S(1)} %get-tuple-element.55), channel_id=1, source_target_pairs={{0,8},{8,16},{16,24},{1,9},{9,17},{17,25},{2,10},{10,18},{18,26},{... | collective-permute-start | bytes 2312 | tf_op jit(solution)/shard_map/ppermute | solution.py:21
  10.6 70.2 %collective-permute-start.5 = (f32[3,32,2]{2,1,0:T(8,128)S(1)}, f32[3,32,2]{2,1,0:T(8,128)S(1)}, u32[]{:S(2)}, u32[]{:S(2)}) collective-permute-start(f32[3,32,2]{2,1,0:T(8,128)S(1)} %get-tuple-element.56), channel_id=1, source_target_pairs={{8,0},{16,8},{24,16},{9,1},{17,9},{25,17},{10,2},{18,10},{26,18},{... | collective-permute-start | bytes 2312 | tf_op jit(solution)/shard_map/ppermute | solution.py:23
  34.9 45.9 %copy-start.9 = (f32[32,128]{1,0:T(8,128)S(1)}, f32[32,128]{1,0:T(8,128)}, u32[]{:S(2)}) copy-start(f32[32,128]{1,0:T(8,128)} %param.19) | copy-start | bytes 49156
  34.9 59.9 %copy-start = (bf16[1,1,4,4,256,256]{5,4,3,2,1,0:T(8,128)(2,1)S(1)}, bf16[1,1,4,4,256,256]{5,4,3,2,1,0:T(8,128)(2,1)}, u32[]{:S(2)}) copy-start(bf16[1,1,4,4,256,256]{5,4,3,2,1,0:T(8,128)(2,1)} %param.15) | copy-start | bytes 6291460
  81.5 69.9 %collective-permute-start.6 = (f32[3,2,132]{2,1,0:T(2,128)}, f32[3,2,132]{2,1,0:T(2,128)}, u32[]{:S(2)}, u32[]{:S(2)}) collective-permute-start(f32[3,2,132]{2,1,0:T(2,128)} %get-tuple-element.41), channel_id=1, source_target_pairs={{0,1},{1,2},{2,3},{3,4},{4,5},{5,6},{6,7},{8,9},{9,10},{10,11},{11... | collective-permute-start | bytes 9512 | tf_op jit(solution)/shard_map/ppermute | solution.py:21
  83.4 68.1 %collective-permute-start.7 = (f32[3,2,132]{2,1,0:T(2,128)}, f32[3,2,132]{2,1,0:T(2,128)}, u32[]{:S(2)}, u32[]{:S(2)}) collective-permute-start(f32[3,2,132]{2,1,0:T(2,128)} %get-tuple-element.42), channel_id=1, source_target_pairs={{1,0},{2,1},{3,2},{4,3},{5,4},{6,5},{7,6},{9,8},{10,9},{11,10},{12... | collective-permute-start | bytes 9512 | tf_op jit(solution)/shard_map/ppermute | solution.py:23
  104.5 9.6 %copy-start.17 = (pred[1024]{0:T(1024)(128)(4,1)S(1)}, pred[1024]{0:T(1024)(128)(4,1)}, u32[]{:S(2)}) copy-start(pred[1024]{0:T(1024)(128)(4,1)} %compare_and_fusion) | copy-start | bytes 3076
  105.6 8.9 %copy-start.18 = (f32[4]{0:T(128)S(1)}, f32[4]{0:T(128)}, u32[]{:S(2)}) copy-start(f32[4]{0:T(128)} %get-tuple-element.69) | copy-start | bytes 52
  114.4 7.6 %copy-start.10 = (s32[1024,1]{0,1:T(1,128)S(1)}, s32[1024,1]{0,1:T(1,128)}, u32[]{:S(2)}) copy-start(s32[1024,1]{0,1:T(1,128)} %compare_select_fusion.2) | copy-start | bytes 12292
  114.8 14.4 %copy-start.11 = (s32[1024,1]{0,1:T(1,128)S(1)}, s32[1024,1]{0,1:T(1,128)}, u32[]{:S(2)}) copy-start(s32[1024,1]{0,1:T(1,128)} %compare_select_fusion.1) | copy-start | bytes 12292
  122.0 14.0 %copy-start.12 = (s32[1024,1]{0,1:T(1,128)S(1)}, s32[1024,1]{0,1:T(1,128)}, u32[]{:S(2)}) copy-start(s32[1024,1]{0,1:T(1,128)} %compare_select_fusion) | copy-start | bytes 12292
  143.0 8.4 %copy-start.6 = (f32[3,32,2]{2,1,0:T(8,128)S(1)}, f32[3,32,2]{2,1,0:T(8,128)}, u32[]{:S(2)}) copy-start(f32[3,32,2]{2,1,0:T(8,128)} %copy-done.5) | copy-start | bytes 2308
  143.0 8.4 %copy-start.8 = (f32[3,32,2]{2,1,0:T(8,128)S(1)}, f32[3,32,2]{2,1,0:T(8,128)}, u32[]{:S(2)}) copy-start(f32[3,32,2]{2,1,0:T(8,128)} %copy-done.7) | copy-start | bytes 2308
  143.0 22.0 %copy-start.15 = (f32[32]{0:T(128)S(1)}, f32[32]{0:T(128)}, u32[]{:S(2)}) copy-start(f32[32]{0:T(128)} %get-tuple-element.73) | copy-start | bytes 388
  143.0 22.0 %copy-start.16 = (f32[32]{0:T(128)S(1)}, f32[32]{0:T(128)}, u32[]{:S(2)}) copy-start(f32[32]{0:T(128)} %get-tuple-element.74) | copy-start | bytes 388
  145.9 6.4 %collective-permute-start = (f32[3,32,2]{2,1,0:T(8,128)S(1)}, f32[3,32,2]{2,1,0:T(8,128)S(1)}, u32[]{:S(2)}, u32[]{:S(2)}) collective-permute-start(f32[3,32,2]{2,1,0:T(8,128)S(1)} %get-tuple-element.53), channel_id=1, source_target_pairs={{0,8},{8,16},{16,24},{1,9},{9,17},{17,25},{2,10},{10,18},{18,26},{... | collective-permute-start | bytes 2312 | tf_op jit(solution)/shard_map/ppermute | solution.py:21
  150.1 6.0 %collective-permute-start.1 = (f32[3,32,2]{2,1,0:T(8,128)S(1)}, f32[3,32,2]{2,1,0:T(8,128)S(1)}, u32[]{:S(2)}, u32[]{:S(2)}) collective-permute-start(f32[3,32,2]{2,1,0:T(8,128)S(1)} %get-tuple-element.54), channel_id=1, source_target_pairs={{8,0},{16,8},{24,16},{9,1},{17,9},{25,17},{10,2},{18,10},{26,18},{... | collective-permute-start | bytes 2312 | tf_op jit(solution)/shard_map/ppermute | solution.py:23
  156.2 4.1 %collective-permute-start.2 = (f32[3,2,132]{2,1,0:T(2,128)S(1)}, f32[3,2,132]{2,1,0:T(2,128)S(1)}, u32[]{:S(2)}, u32[]{:S(2)}) collective-permute-start(f32[3,2,132]{2,1,0:T(2,128)S(1)} %get-tuple-element.39), channel_id=1, source_target_pairs={{0,1},{1,2},{2,3},{3,4},{4,5},{5,6},{6,7},{8,9},{9,10},{10,11},{11... | collective-permute-start | bytes 9512 | tf_op jit(solution)/shard_map/ppermute | solution.py:21
  159.0 5.7 %collective-permute-start.3 = (f32[3,2,132]{2,1,0:T(2,128)S(1)}, f32[3,2,132]{2,1,0:T(2,128)S(1)}, u32[]{:S(2)}, u32[]{:S(2)}) collective-permute-start(f32[3,2,132]{2,1,0:T(2,128)S(1)} %get-tuple-element.40), channel_id=1, source_target_pairs={{1,0},{2,1},{3,2},{4,3},{5,4},{6,5},{7,6},{9,8},{10,9},{11,10},{12... | collective-permute-start | bytes 9512 | tf_op jit(solution)/shard_map/ppermute | solution.py:23
  165.8 6.2 %collective-permute-start.8 = (f32[3,32,2]{2,1,0:T(8,128)S(1)}, f32[3,32,2]{2,1,0:T(8,128)S(1)}, u32[]{:S(2)}, u32[]{:S(2)}) collective-permute-start(f32[3,32,2]{2,1,0:T(8,128)S(1)} %get-tuple-element.51), channel_id=1, source_target_pairs={{0,8},{8,16},{16,24},{1,9},{9,17},{17,25},{2,10},{10,18},{18,26},{... | collective-permute-start | bytes 2312 | tf_op jit(solution)/shard_map/ppermute | solution.py:21
  170.3 6.0 %collective-permute-start.9 = (f32[3,32,2]{2,1,0:T(8,128)S(1)}, f32[3,32,2]{2,1,0:T(8,128)S(1)}, u32[]{:S(2)}, u32[]{:S(2)}) collective-permute-start(f32[3,32,2]{2,1,0:T(8,128)S(1)} %get-tuple-element.52), channel_id=1, source_target_pairs={{8,0},{16,8},{24,16},{9,1},{17,9},{25,17},{10,2},{18,10},{26,18},{... | collective-permute-start | bytes 2312 | tf_op jit(solution)/shard_map/ppermute | solution.py:23
  176.4 46.8 %collective-permute-start.10 = (f32[3,2,132]{2,1,0:T(2,128)S(1)}, f32[3,2,132]{2,1,0:T(2,128)S(1)}, u32[]{:S(2)}, u32[]{:S(2)}) collective-permute-start(f32[3,2,132]{2,1,0:T(2,128)S(1)} %get-tuple-element.37), channel_id=1, source_target_pairs={{0,1},{1,2},{2,3},{3,4},{4,5},{5,6},{6,7},{8,9},{9,10},{10,11},{11... | collective-permute-start | bytes 9512 | tf_op jit(solution)/shard_map/ppermute | solution.py:21
  179.2 44.0 %collective-permute-start.11 = (f32[3,2,132]{2,1,0:T(2,128)S(1)}, f32[3,2,132]{2,1,0:T(2,128)S(1)}, u32[]{:S(2)}, u32[]{:S(2)}) collective-permute-start(f32[3,2,132]{2,1,0:T(2,128)S(1)} %get-tuple-element.38), channel_id=1, source_target_pairs={{1,0},{2,1},{3,2},{4,3},{5,4},{6,5},{7,6},{9,8},{10,9},{11,10},{12... | collective-permute-start | bytes 9512 | tf_op jit(solution)/shard_map/ppermute | solution.py:23
  224.3 5.9 %collective-permute-start.12 = (f32[3,32,2]{2,1,0:T(8,128)S(1)}, f32[3,32,2]{2,1,0:T(8,128)S(1)}, u32[]{:S(2)}, u32[]{:S(2)}) collective-permute-start(f32[3,32,2]{2,1,0:T(8,128)S(1)} %get-tuple-element.49), channel_id=1, source_target_pairs={{0,8},{8,16},{16,24},{1,9},{9,17},{17,25},{2,10},{10,18},{18,26},{... | collective-permute-start | bytes 2312 | tf_op jit(solution)/shard_map/ppermute | solution.py:21
  228.5 6.0 %collective-permute-start.13 = (f32[3,32,2]{2,1,0:T(8,128)S(1)}, f32[3,32,2]{2,1,0:T(8,128)S(1)}, u32[]{:S(2)}, u32[]{:S(2)}) collective-permute-start(f32[3,32,2]{2,1,0:T(8,128)S(1)} %get-tuple-element.50), channel_id=1, source_target_pairs={{8,0},{16,8},{24,16},{9,1},{17,9},{25,17},{10,2},{18,10},{26,18},{... | collective-permute-start | bytes 2312 | tf_op jit(solution)/shard_map/ppermute | solution.py:23
  234.5 45.0 %collective-permute-start.14 = (f32[3,2,132]{2,1,0:T(2,128)S(1)}, f32[3,2,132]{2,1,0:T(2,128)S(1)}, u32[]{:S(2)}, u32[]{:S(2)}) collective-permute-start(f32[3,2,132]{2,1,0:T(2,128)S(1)} %get-tuple-element.35), channel_id=1, source_target_pairs={{0,1},{1,2},{2,3},{3,4},{4,5},{5,6},{6,7},{8,9},{9,10},{10,11},{11... | collective-permute-start | bytes 9512 | tf_op jit(solution)/shard_map/ppermute | solution.py:21
  235.8 43.7 %collective-permute-start.15 = (f32[3,2,132]{2,1,0:T(2,128)S(1)}, f32[3,2,132]{2,1,0:T(2,128)S(1)}, u32[]{:S(2)}, u32[]{:S(2)}) collective-permute-start(f32[3,2,132]{2,1,0:T(2,128)S(1)} %get-tuple-element.36), channel_id=1, source_target_pairs={{1,0},{2,1},{3,2},{4,3},{5,4},{6,5},{7,6},{9,8},{10,9},{11,10},{12... | collective-permute-start | bytes 9512 | tf_op jit(solution)/shard_map/ppermute | solution.py:23
  280.6 5.9 %collective-permute-start.16 = (f32[3,32,2]{2,1,0:T(8,128)S(1)}, f32[3,32,2]{2,1,0:T(8,128)S(1)}, u32[]{:S(2)}, u32[]{:S(2)}) collective-permute-start(f32[3,32,2]{2,1,0:T(8,128)S(1)} %get-tuple-element.47), channel_id=1, source_target_pairs={{0,8},{8,16},{16,24},{1,9},{9,17},{17,25},{2,10},{10,18},{18,26},{... | collective-permute-start | bytes 2312 | tf_op jit(solution)/shard_map/ppermute | solution.py:21
  284.8 6.0 %collective-permute-start.17 = (f32[3,32,2]{2,1,0:T(8,128)S(1)}, f32[3,32,2]{2,1,0:T(8,128)S(1)}, u32[]{:S(2)}, u32[]{:S(2)}) collective-permute-start(f32[3,32,2]{2,1,0:T(8,128)S(1)} %get-tuple-element.48), channel_id=1, source_target_pairs={{8,0},{16,8},{24,16},{9,1},{17,9},{25,17},{10,2},{18,10},{26,18},{... | collective-permute-start | bytes 2312 | tf_op jit(solution)/shard_map/ppermute | solution.py:23
  290.9 47.8 %collective-permute-start.18 = (f32[3,2,132]{2,1,0:T(2,128)S(1)}, f32[3,2,132]{2,1,0:T(2,128)S(1)}, u32[]{:S(2)}, u32[]{:S(2)}) collective-permute-start(f32[3,2,132]{2,1,0:T(2,128)S(1)} %get-tuple-element.33), channel_id=1, source_target_pairs={{0,1},{1,2},{2,3},{3,4},{4,5},{5,6},{6,7},{8,9},{9,10},{10,11},{11... | collective-permute-start | bytes 9512 | tf_op jit(solution)/shard_map/ppermute | solution.py:21
  292.2 46.5 %collective-permute-start.19 = (f32[3,2,132]{2,1,0:T(2,128)S(1)}, f32[3,2,132]{2,1,0:T(2,128)S(1)}, u32[]{:S(2)}, u32[]{:S(2)}) collective-permute-start(f32[3,2,132]{2,1,0:T(2,128)S(1)} %get-tuple-element.34), channel_id=1, source_target_pairs={{1,0},{2,1},{3,2},{4,3},{5,4},{6,5},{7,6},{9,8},{10,9},{11,10},{12... | collective-permute-start | bytes 9512 | tf_op jit(solution)/shard_map/ppermute | solution.py:23
  (10 other events, 47.7 us)
where the time goes:
time: 341 us; the launch traced here: 340 us
  blocking collectives  188 us (55%)
  starting transfers between devices  49.1 us (14%)
  other arithmetic  45 us (13%)
  local copies, waits for them, and re-layouts  28.6 us (8%)
  waiting for transfers between devices  22.3 us (7%)
  between operations  4.32 us (1%)
    pmax x4, blocking collectives, shards(): fastest = lax.pmax(local_speed, ('comp', 'dom'))  166 us
    ppermute x10, starting transfers between devices, padded(): lax.ppermute(tail, axis, [(i, (i + 1) % count) for i in range(ends)])  31 us
    scatter-add x4, other arithmetic, deposit(): return total.at[:, targets.reshape(-1)].add(flat)  27.9 us
    all_gather x1, blocking collectives, shards(): piece = lax.all_gather(atm_fields, 'comp', axis=1, tiled=True)  21.7 us
    ppermute x10, waiting for transfers between devices, padded(): lax.ppermute(head, axis, [((i + 1) % count, i) for i in range(ends)])  21 us
    gather x4, local copies, waits for them, and re-layouts, shards(): jnp.take(section, columns.reshape(-1), axis=1)  17.8 us
    ppermute x10, starting transfers between devices, padded(): lax.ppermute(head, axis, [((i + 1) % count, i) for i in range(ends)])  12.9 us
  transfers between devices with their start and end apart: 21, of which 8 were waited for; matrix products, arithmetic and copies ran while one was open for 21% of the time, Pallas kernels for 0%

commit v1 on v0

v1 whole, which is shorter than its diff:
```python
import functools

import jax
import jax.numpy as jnp
from jax import lax
from jax.experimental import pallas as pl
from jax.experimental.pallas import tpu as pltpu
from jax.sharding import PartitionSpec as P

NSUB = 4
HALO = 2 * NSUB
LANES = 128

courant = 0.5
friction = 0.05

MESH = pl.DeviceIdType.MESH
COMPASS = [(-1, 0), (1, 0), (0, 1), (0, -1), (1, 1), (-1, 1), (1, -1), (-1, -1)]


def nt_dot(a, b):
    return lax.dot_general(a, b, (((1,), (1,)), ((), ())), preferred_element_type=jnp.float32)


def log2(n):
    assert n & (n - 1) == 0
    return n.bit_length() - 1


def pack_edges(fields):
    slot = lax.broadcasted_iota(jnp.int32, fields[0].shape, 1) // (2 * HALO)
    packed = jnp.zeros_like(fields[0])
    for i, field in enumerate(fields):
        packed = jnp.where(slot == i, pltpu.roll(field, 2 * HALO * i + HALO, 1), packed)
    return packed


def gather_kernel(
    atm_ref, cols_ref, live_ref, map_ref, depth_ref, wet_ref, level_ref, east_ref, north_ref,
    out_ref, target_ref, init_ref, edges_ref, speed_ref, wide,
):
    nfield, ncol = atm_ref.shape
    ngroup, capacity, width = cols_ref.shape
    dead = depth_ref.shape[0] * depth_ref.shape[1]
    wide[...] = atm_ref[...].astype(jnp.float32)

    wet = wet_ref[...].astype(jnp.float32)
    fields = [level_ref[...], east_ref[...], north_ref[...], depth_ref[...], wet]
    for i, field in enumerate(fields):
        init_ref[i] = field
    edges_ref[...] = pack_edges(fields)
    speed = jnp.sqrt(fields[3]) + wet * (jnp.abs(fields[1]) + jnp.abs(fields[2]))
    speed_ref[...] = jnp.max(speed, axis=0, keepdims=True)

    slot = lax.broadcasted_iota(jnp.int32, (capacity, width), 0)
    for s in range(ngroup):
        target_ref[s] = jnp.where(slot < live_ref[s], map_ref[s], dead)

    def group(g, carry):
        lists = cols_ref[g]
        for part in range(width // LANES):
            rows = []
            for k in range(capacity):
                index = lists[k : k + 1, part * LANES : (part + 1) * LANES]
                index = jnp.broadcast_to(index, (nfield, LANES))
                high = index >> log2(LANES)
                low = index & (LANES - 1)
                value = jnp.zeros((nfield, LANES), jnp.float32)
                for c in range(ncol // LANES):
                    chunk = wide[:, c * LANES : (c + 1) * LANES]
                    taken = jnp.take_along_axis(chunk, low, axis=1, mode="promise_in_bounds")
                    value = jnp.where(high == c, taken, value)
                rows.append(value)
            out_ref[g, :, part * LANES : (part + 1) * LANES] = jnp.concatenate(rows, 0).astype(
                out_ref.dtype
            )
        return carry

    lax.fori_loop(0, ngroup, group, 0)


def ocean_kernel(
    nc, nd,
    blocks_ref, target_ref, init_ref, edges_ref, speed_ref, weights_hbm,
    flux_hbm, state_ref,
    weights, arrived, contrib, acc, flux, push_edges, rows_in, side_in, push_rows_in, push_side_in,
    fast, fastest,
    weight_sem, flux_sem, block_send, block_recv, halo_send, halo_recv, fast_send, fast_recv,
):
    me_c, me_d = lax.axis_index("comp"), lax.axis_index("dom")
    nfield, nrows, ncols = flux.shape
    capacity, width = target_ref.shape[1:]
    half = nrows // 2
    total = nc * nd

    def weight_copy(offset):
        source = lax.rem(me_c + nc - offset, nc)
        return pltpu.make_async_copy(
            weights_hbm.at[source], weights.at[offset], weight_sem.at[offset]
        )

    def others(act):
        for dc in range(nc):
            c = lax.rem(me_c + dc, nc)

            def one(dd, carry, dc=dc, c=c):
                d = lax.rem(me_d + dd, nd)
                act(dc * nd + dd - 1, (c, d))
                return carry

            lax.fori_loop(1 if dc == 0 else 0, nd, one, 0)

    barrier = pltpu.get_barrier_semaphore()
    others(
        lambda slot, device: pl.semaphore_signal(
            barrier, inc=1, device_id=device, device_id_type=MESH
        )
    )
    for offset in range(nc):
        weight_copy(offset).start()

    def send_fast(turn, src):
        def act(slot, device):
            pltpu.make_async_remote_copy(
                src_ref=src,
                dst_ref=fastest.at[turn, slot],
                send_sem=fast_send.at[turn],
                recv_sem=fast_recv.at[turn],
                device_id=device,
                device_id_type=MESH,
            ).start()

        others(act)

    def wait_fast(turn):
        pltpu.make_async_copy(fastest.at[turn], fastest.at[turn], fast_recv.at[turn]).wait()

    def halo_refs(step, rows, edges, rows_into, side_into):
        dr, dc = step
        side = (0 if dc > 0 else 1) if dc else (0 if dr > 0 else 1)
        near = pl.ds(nrows - HALO, HALO) if dr > 0 else pl.ds(0, HALO)
        if dc == 0:
            return rows.at[:, near, :], rows_into.at[side]
        if dr == 0:
            return edges, side_into.at[side, pl.ds(HALO, nrows), :]
        far = pl.ds(0, HALO) if dr > 0 else pl.ds(HALO + nrows, HALO)
        return edges.at[near, :], side_into.at[side, far, :]

    def inside(c, d):
        return (c >= 0) & (c < nc) & (d >= 0) & (d < nd)

    def send_halo(turn, *refs):
        for i, step in enumerate(COMPASS):
            src, dst = halo_refs(step, *refs)
            c, d = me_c + step[1], me_d + step[0]

            @pl.when(inside(c, d))
            def _(i=i, src=src, dst=dst, c=c, d=d):
                pltpu.make_async_remote_copy(
                    src_ref=src,
                    dst_ref=dst,
                    send_sem=halo_send.at[turn, i],
                    recv_sem=halo_recv.at[turn, i],
                    device_id=(c, d),
                    device_id_type=MESH,
                ).start()

    def clear_halo(*refs):
        for step in COMPASS:
            _, dst = halo_refs(step, *refs)

            @pl.when(jnp.logical_not(inside(me_c - step[1], me_d - step[0])))
            def _(dst=dst):
                dst[...] = jnp.zeros(dst.shape, dst.dtype)

    def wait_halo(turn, *refs):
        for i, step in enumerate(COMPASS):
            _, dst = halo_refs(step, *refs)

            @pl.when(inside(me_c - step[1], me_d - step[0]))
            def _(i=i, dst=dst):
                pltpu.make_async_copy(dst, dst, halo_recv.at[turn, i]).wait()

    def drain_halo(turn, *refs):
        for i, step in enumerate(COMPASS):
            src, _ = halo_refs(step, *refs)

            @pl.when(inside(me_c + step[1], me_d + step[0]))
            def _(i=i, src=src):
                pltpu.make_async_copy(src, src, halo_send.at[turn, i]).wait()

    def block_copy(offset):
        peer = lax.rem(me_c + offset, nc)
        return pltpu.make_async_remote_copy(
            src_ref=blocks_ref.at[peer],
            dst_ref=arrived.at[offset - 1],
            send_sem=block_send.at[offset - 1],
            recv_sem=block_recv.at[offset - 1],
            device_id=(peer, me_d),
            device_id_type=MESH,
        )

    key_iota = lax.broadcasted_iota(jnp.int32, (2 * ncols, width), 0)
    row_iota = lax.broadcasted_iota(jnp.int32, (half, width), 0)

    def deposit(offset):
        source = lax.rem(me_c + nc - offset, nc)
        blocks = blocks_ref[source] if offset == 0 else arrived[offset - 1]
        for k in range(capacity):
            product = nt_dot(blocks, weights[offset, k])
            contrib[k] = product[k * nfield : (k + 1) * nfield]

        targets = target_ref[source]
        for k in range(capacity):
            target = targets[k : k + 1, :]
            row = target >> log2(ncols)
            key = ((row >> log2(half)) << log2(ncols)) + (target & (ncols - 1))
            group = row & (half - 1)
            chosen = jnp.where(key_iota == key, 1.0, 0.0).astype(jnp.bfloat16)
            where_row = jnp.where(row_iota == group, 1.0, 0.0)
            spread = (contrib[k][:, None, :] * where_row[None]).reshape(nfield * half, width)
            top = spread.astype(jnp.bfloat16)
            rest = (spread - top.astype(jnp.float32)).astype(jnp.bfloat16)
            update = nt_dot(top, chosen) + nt_dot(rest, chosen)
            if offset == 0 and k == 0:
                acc[...] = update
            else:
                acc[...] += update

    first = (init_ref, edges_ref, rows_in, side_in)
    second = (flux.at[pl.ds(0, 3)], push_edges, push_rows_in, push_side_in)
    clear_halo(*first)
    clear_halo(*second)
    weight_copy(0).wait()
    deposit(0)

    pl.semaphore_wait(barrier, total - 1)
    for offset in range(1, nc):
        block_copy(offset).start()
    send_halo(0, *first)
    send_fast(0, speed_ref)

    for offset in range(1, nc):
        weight_copy(offset).wait()
        block_copy(offset).wait_recv()
        deposit(offset)

    pushes = []
    for f in range(nfield):
        upper = acc[f * half : (f + 1) * half, :ncols]
        lower = acc[f * half : (f + 1) * half, ncols:]
        flux[f, :half] = upper
        flux[f, half:] = lower
        if f < 3:
            pushes.append(jnp.concatenate([upper, lower], 0))
        if f == 2:
            push_edges[...] = pack_edges(pushes)
    send_halo(1, *second)
    flux_copy = pltpu.make_async_copy(flux, flux_hbm, flux_sem)
    flux_copy.start()

    high = nrows + 2 * HALO
    lane = lax.broadcasted_iota(jnp.int32, (high, ncols), 1)
    beside = (lane < HALO) | (lane >= ncols - HALO)
    west_part = (lane & (2 * HALO - 1)) < HALO

    def extended(i, center, rows, mixed):
        main = jnp.concatenate([rows[0, i], center, rows[1, i]], 0)
        side = pltpu.roll(mixed, ncols - (2 * HALO * i + HALO), 1)
        return jnp.concatenate([main, jnp.where(beside, side, 0.0)], 1)

    wait_halo(0, *first)
    mixed = jnp.where(west_part, side_in[0], side_in[1])
    level, east, north, depth, wet = [
        extended(i, init_ref[i], rows_in, mixed) for i in range(5)
    ]
    root_depth = jnp.sqrt(init_ref[3])
    wet_here = init_ref[4]
    conduct = depth * wet
    some_depth = jnp.where(depth > 0.0, depth, 1.0)
    global_row = (
        lax.broadcasted_iota(jnp.int32, (high, 2 * ncols), 0) + (me_d * nrows - HALO)
    ).astype(jnp.float32)
    rotation = 0.1 + 0.4 * (global_row + 0.5) / (nrows * nd)

    def across(x):
        return pltpu.roll(x, 2 * ncols - 1, 1) - pltpu.roll(x, 1, 1)

    def along(x):
        return pltpu.roll(x, high - 1, 0) - pltpu.roll(x, 1, 0)

    wait_halo(1, *second)
    mixed = jnp.where(west_part, push_side_in[0], push_side_in[1])
    push_x, push_y, fresh = [
        extended(i, flux[i], push_rows_in, mixed) for i in range(3)
    ]
    push_x = push_x / some_depth
    push_y = push_y / some_depth

    for turn in range(NSUB):
        own = speed_ref if turn == 0 else fast.at[turn - 1]
        diverge = 0.5 * (across(conduct * east) + along(conduct * north))
        wait_fast(turn)
        peak = jnp.maximum(jnp.max(fastest[turn], axis=0), own[...])
        step_dt = courant / jnp.max(peak, axis=1, keepdims=True)
        level = wet * (level + step_dt * (fresh - diverge))
        east, north = (
            wet * (east + step_dt * (rotation * north - 0.5 * across(level) + push_x - friction * east)),
            wet * (north + step_dt * (-rotation * east - 0.5 * along(level) + push_y - friction * north)),
        )
        if turn < NSUB - 1:
            near_east = east[HALO : HALO + nrows, :ncols]
            near_north = north[HALO : HALO + nrows, :ncols]
            speed = root_depth + wet_here * (jnp.abs(near_east) + jnp.abs(near_north))
            fast[turn] = jnp.max(speed, axis=0, keepdims=True)
            send_fast(turn + 1, fast.at[turn])

    for i, value in enumerate((level, east, north)):
        state_ref[i] = value[HALO : HALO + nrows, :ncols]

    for offset in range(1, nc):
        block_copy(offset).wait_send()
    drain_halo(0, *first)
    drain_halo(1, *second)
    for turn in range(NSUB):
        pltpu.make_async_copy(fastest.at[turn], fastest.at[turn], fast_send.at[turn]).wait()
    flux_copy.wait()


def shards(
    nc, nd,
    atm_fields, send_cols, live_blocks, remap_weights, row_map,
    ocean_depth, wet_mask, sea_level, east_vel, north_vel,
):
    nfield, ncol = atm_fields.shape
    ngroup, capacity, width = send_cols.shape[2:]
    nrows, ncols = ocean_depth.shape
    f32, bf16 = jnp.float32, jnp.bfloat16
    vmem = pl.BlockSpec(memory_space=pltpu.VMEM)
    smem = pl.BlockSpec(memory_space=pltpu.SMEM)
    anywhere = pl.BlockSpec(memory_space=pl.ANY)

    blocks, targets, init, edges, speed = pl.pallas_call(
        gather_kernel,
        name="gather_columns",
        out_shape=(
            jax.ShapeDtypeStruct((ngroup, capacity * nfield, width), bf16),
            jax.ShapeDtypeStruct((ngroup, capacity, width), jnp.int32),
            jax.ShapeDtypeStruct((5, nrows, ncols), f32),
            jax.ShapeDtypeStruct((nrows, ncols), f32),
            jax.ShapeDtypeStruct((1, ncols), f32),
        ),
        in_specs=[vmem, vmem, smem] + [vmem] * 6,
        out_specs=[vmem] * 5,
        scratch_shapes=[pltpu.VMEM((nfield, ncol), f32)],
    )(
        atm_fields, send_cols[0, 0], live_blocks[0, 0], row_map[0, 0],
        ocean_depth, wet_mask, sea_level, east_vel, north_vel,
    )

    high = nrows + 2 * HALO
    dma = pltpu.SemaphoreType.DMA
    fluxes, state = pl.pallas_call(
        functools.partial(ocean_kernel, nc, nd),
        name="remap_and_step",
        out_shape=(
            jax.ShapeDtypeStruct((nfield, nrows, ncols), f32),
            jax.ShapeDtypeStruct((3, nrows, ncols), f32),
        ),
        in_specs=[vmem] * 5 + [anywhere],
        out_specs=[anywhere, vmem],
        scratch_shapes=[
            pltpu.VMEM((nc, capacity, width, width), bf16),
            pltpu.VMEM((nc - 1, capacity * nfield, width), bf16),
            pltpu.VMEM((capacity, nfield, width), f32),
            pltpu.VMEM((nfield * nrows // 2, 2 * ncols), f32),
            pltpu.VMEM((nfield, nrows, ncols), f32),
            pltpu.VMEM((nrows, ncols), f32),
            pltpu.VMEM((2, 5, HALO, ncols), f32),
            pltpu.VMEM((2, high, ncols), f32),
            pltpu.VMEM((2, 3, HALO, ncols), f32),
            pltpu.VMEM((2, high, ncols), f32),
            pltpu.VMEM((NSUB - 1, 1, ncols), f32),
            pltpu.VMEM((NSUB, nc * nd - 1, 1, ncols), f32),
            dma((nc,)),
            dma(()),
            dma((nc - 1,)),
            dma((nc - 1,)),
            dma((2, 8)),
            dma((2, 8)),
            dma((NSUB,)),
            dma((NSUB,)),
        ],
        compiler_params=pltpu.CompilerParams(collective_id=0, has_side_effects=True),
    )(blocks, targets, init, edges, speed, remap_weights[0, 0])
    return fluxes, state


def solution(mesh):
    in_specs = (
        P(None, ("comp", "dom")),
        P("comp", "dom", None, None, None),
        P("comp", "dom", None),
        P("comp", "dom", None, None, None, None),
        P("comp", "dom", None, None, None),
        P("dom", "comp"),
        P("dom", "comp"),
        P("dom", "comp"),
        P("dom", "comp"),
        P("dom", "comp"),
    )
    out_specs = (P(None, "dom", "comp"), P(None, "dom", "comp"))
    body = functools.partial(shards, mesh.shape["comp"], mesh.shape["dom"])
    return jax.shard_map(body, mesh=mesh, in_specs=in_specs, out_specs=out_specs, check_vma=False)
```

time: 341 us -> 40.6 us (0.12)
  blocking collectives: 188 us -> 0 us
  starting transfers between devices: 49.1 us -> 0 us
  other arithmetic: 45 us -> 0 us
  Pallas kernels: 0 us -> 36.4 us
  local copies, waits for them, and re-layouts: 28.6 us -> 3.19 us
  waiting for transfers between devices: 22.3 us -> 0 us
  between operations: 4.32 us -> 0.64 us
    pmax x4 -> x0, blocking collectives: 166 us -> none  [shards(): fastest = lax.pmax(local_speed, ('comp', 'dom'))]
    ppermute x20 -> x0, starting transfers between devices: 43.9 us -> none  [the longest x10 31 us: padded(): lax.ppermute(tail, axis, [(i, (i + 1) % count) for i in range(ends)])]
    pallas_call x0 -> x2, Pallas kernels: none -> 36.4 us  [the longest x1 33.5 us: shards(): pl.pallas_call(functools.partial(ocean_kernel, nc, nd), name='remap_and_s...]
    scatter-add x4 -> x0, other arithmetic: 27.9 us -> none  [deposit(): return total.at[:, targets.reshape(-1)].add(flat)]
    ppermute x20 -> x0, waiting for transfers between devices: 22.3 us -> none  [the longest x10 21 us: padded(): lax.ppermute(head, axis, [((i + 1) % count, i) for i in range(ends)])]
    all_gather x1 -> x0, blocking collectives: 21.7 us -> none  [shards(): piece = lax.all_gather(atm_fields, 'comp', axis=1, tiled=True)]
    gather x4 -> x0, local copies, waits for them, and re-layouts: 17.8 us -> none  [shards(): jnp.take(section, columns.reshape(-1), axis=1)]
    select_n x8 -> x0, other arithmetic: 5.77 us -> none  [the longest x4 3.37 us: shards(): jnp.take(section, columns.reshape(-1), axis=1)]
  transfers between devices with their start and end apart: 21 -> 0, of which waited for: 8 -> 0; matrix products, arithmetic and copies ran while one was open for 21% -> 0% of each run, Pallas kernels for 0% -> 0%
where the time goes in v1:
time: 40.6 us; the launch traced here: 40.3 us
  Pallas kernels  36.4 us (90%)
  local copies, waits for them, and re-layouts  3.19 us (8%)
  between operations  0.64 us (2%)
    pallas_call x1, Pallas kernels, shards(): pl.pallas_call(functools.partial(ocean_kernel, nc, nd), name='remap_and_s...  33.5 us
    unnamed x2, local copies, waits for them, and re-layouts  3.19 us
    pallas_call x1, Pallas kernels, shards(): pl.pallas_call(gather_kernel, name='gather_columns', out_shape=(jax.Shape...  2.93 us

profile of v1, /device:TPU:0, one launch (start us, length us, event | category | flops | bytes accessed | tf_op | source)
XLA Modules:
  0.0 40.3 jit_solution(10211903521737711792)
XLA Ops:
  0.6 2.9 %gather_columns.1 = (bf16[4,96,256]{2,1,0:T(8,128)(2,1)}, s32[4,4,256]{2,1,0:T(4,128)}, f32[5,32,128]{2,1,0:T(8,128)}, f32[32,128]{1,0:T(8,128)}, f32[1,128]{1,0:T(1,128)}) custom-call(bf16[24,2048]{1,0:T(8,128)(2,1)} %atm_ref.1, s32[4,4,256]{2,1,0:T(4,128)} %bitcast.5, s32[4]{0:T(128)} %bitcast.7, s32[4,4,256]{2,1,0:T(4,128)} %bitcast.6, ...), custom_call_target="tpu_custom_call" | custom-call | tf_op jit(solution)/shard_map/gather_columns/pallas_call | solution.py:343
  3.6 33.5 %remap_and_step.1 = (f32[24,32,128]{2,1,0:T(8,128)}, f32[3,32,128]{2,1,0:T(8,128)}) custom-call(bf16[4,96,256]{2,1,0:T(8,128)(2,1)} %get-tuple-element.7.blocks_ref, s32[4,4,256]{2,1,0:T(4,128)} %get-tuple-element.8.target_ref, f32[5,32,128]{2,1,0:T(8,128)} %get-tuple-element.9.init_ref, f32[32,128]{1,0:T(8,128)} %get-tuple-element.10.edges_ref, ...), custom_call_target="tpu_custom_call" | custom-call | tf_op jit(solution)/shard_map/remap_and_step/pallas_call | solution.py:363
  37.1 1.8 %copy.14 = f32[24,32,128]{2,1,0:T(8,128)} copy(f32[24,32,128]{2,1,0:T(8,128)} %get-tuple-element.14) | data formatting | bytes 786432
  38.8 1.4 %copy.15 = f32[3,32,128]{2,1,0:T(8,128)} copy(f32[3,32,128]{2,1,0:T(8,128)} %get-tuple-element.15) | data formatting | bytes 98304

commit v2 on v1

--- a/solution.py
+++ b/solution.py
@@ -35,57 +35,26 @@
     return packed
 
 
-def gather_kernel(
-    atm_ref, cols_ref, live_ref, map_ref, depth_ref, wet_ref, level_ref, east_ref, north_ref,
-    out_ref, target_ref, init_ref, edges_ref, speed_ref, wide,
-):
-    nfield, ncol = atm_ref.shape
-    ngroup, capacity, width = cols_ref.shape
-    dead = depth_ref.shape[0] * depth_ref.shape[1]
-    wide[...] = atm_ref[...].astype(jnp.float32)
-
-    wet = wet_ref[...].astype(jnp.float32)
-    fields = [level_ref[...], east_ref[...], north_ref[...], depth_ref[...], wet]
-    for i, field in enumerate(fields):
-        init_ref[i] = field
-    edges_ref[...] = pack_edges(fields)
-    speed = jnp.sqrt(fields[3]) + wet * (jnp.abs(fields[1]) + jnp.abs(fields[2]))
-    speed_ref[...] = jnp.max(speed, axis=0, keepdims=True)
-
-    slot = lax.broadcasted_iota(jnp.int32, (capacity, width), 0)
-    for s in range(ngroup):
-        target_ref[s] = jnp.where(slot < live_ref[s], map_ref[s], dead)
-
-    def group(g, carry):
-        lists = cols_ref[g]
-        for part in range(width // LANES):
-            rows = []
-            for k in range(capacity):
-                index = lists[k : k + 1, part * LANES : (part + 1) * LANES]
-                index = jnp.broadcast_to(index, (nfield, LANES))
-                high = index >> log2(LANES)
-                low = index & (LANES - 1)
-                value = jnp.zeros((nfield, LANES), jnp.float32)
-                for c in range(ncol // LANES):
-                    chunk = wide[:, c * LANES : (c + 1) * LANES]
-                    taken = jnp.take_along_axis(chunk, low, axis=1, mode="promise_in_bounds")
-                    value = jnp.where(high == c, taken, value)
-                rows.append(value)
-            out_ref[g, :, part * LANES : (part + 1) * LANES] = jnp.concatenate(rows, 0).astype(
-                out_ref.dtype
-            )
-        return carry
-
-    lax.fori_loop(0, ngroup, group, 0)
+def write_out(flux_ref, state_ref, flux_out, state_out, sems):
+    copies = [
+        pltpu.make_async_copy(flux_ref, flux_out, sems.at[0]),
+        pltpu.make_async_copy(state_ref, state_out, sems.at[1]),
+    ]
+    for copy in copies:
+        copy.start()
+    for copy in copies:
+        copy.wait()
 
 
 def ocean_kernel(
     nc, nd,
-    blocks_ref, target_ref, init_ref, edges_ref, speed_ref, weights_hbm,
-    flux_hbm, state_ref,
-    weights, arrived, contrib, acc, flux, push_edges, rows_in, side_in, push_rows_in, push_side_in,
+    atm_ref, cols_ref, live_ref, map_ref, depth_ref, wet_ref, level_ref, east_ref, north_ref,
+    weights_hbm,
+    flux, state_ref,
+    wide, blocks_ref, target_ref, init_ref, edges_ref, speed_ref,
+    weights, arrived, acc, push_edges, rows_in, side_in, push_rows_in, push_side_in,
     fast, fastest,
-    weight_sem, flux_sem, block_send, block_recv, halo_send, halo_recv, fast_send, fast_recv,
+    weight_sem, block_send, block_recv, halo_send, halo_recv, fast_send, fast_recv,
 ):
     me_c, me_d = lax.axis_index("comp"), lax.axis_index("dom")
     nfield, nrows, ncols = flux.shape
@@ -192,7 +161,7 @@
     def block_copy(offset):
         peer = lax.rem(me_c + offset, nc)
         return pltpu.make_async_remote_copy(
-            src_ref=blocks_ref.at[peer],
+            src_ref=blocks_ref.at[offset],
             dst_ref=arrived.at[offset - 1],
             send_sem=block_send.at[offset - 1],
             recv_sem=block_recv.at[offset - 1],
@@ -200,39 +169,69 @@
             device_id_type=MESH,
         )
 
+    wide[...] = atm_ref[...].astype(jnp.float32)
+    wetness = wet_ref[...].astype(jnp.float32)
+    fields = [level_ref[...], east_ref[...], north_ref[...], depth_ref[...], wetness]
+    for i, field in enumerate(fields):
+        init_ref[i] = field
+    edges_ref[...] = pack_edges(fields)
+    speed = jnp.sqrt(fields[3]) + wetness * (jnp.abs(fields[1]) + jnp.abs(fields[2]))
+    speed_ref[...] = jnp.max(speed, axis=0, keepdims=True)
+
+    slot = lax.broadcasted_iota(jnp.int32, (capacity, width), 0)
+    for s in range(nc):
+        target_ref[s] = jnp.where(slot < live_ref[s], map_ref[s], nrows * ncols)
+
+    def gather(offset, carry):
+        lists = cols_ref[lax.rem(me_c + offset, nc)]
+        for part in range(width // LANES):
+            picked = []
+            for k in range(capacity):
+                index = lists[k : k + 1, part * LANES : (part + 1) * LANES]
+                index = jnp.broadcast_to(index, (nfield, LANES))
+                high_bits = index >> log2(LANES)
+                low_bits = index & (LANES - 1)
+                value = jnp.zeros((nfield, LANES), jnp.float32)
+                for c in range(wide.shape[1] // LANES):
+                    chunk = wide[:, c * LANES : (c + 1) * LANES]
+                    taken = jnp.take_along_axis(chunk, low_bits, axis=1, mode="promise_in_bounds")
+                    value = jnp.where(high_bits == c, taken, value)
+                picked.append(value)
+            blocks_ref[offset, :, part * LANES : (part + 1) * LANES] = jnp.concatenate(
+                picked, 0
+            ).astype(blocks_ref.dtype)
+        return carry
+
     key_iota = lax.broadcasted_iota(jnp.int32, (2 * ncols, width), 0)
     row_iota = lax.broadcasted_iota(jnp.int32, (half, width), 0)
 
     def deposit(offset):
         source = lax.rem(me_c + nc - offset, nc)
-        blocks = blocks_ref[source] if offset == 0 else arrived[offset - 1]
+        blocks = blocks_ref[0] if offset == 0 else arrived[offset - 1]
+        targets = target_ref[source]
+        tops, rests, keys = [], [], []
         for k in range(capacity):
-            product = nt_dot(blocks, weights[offset, k])
-            contrib[k] = product[k * nfield : (k + 1) * nfield]
-
-        targets = target_ref[source]
-        for k in range(capacity):
+            product = nt_dot(blocks, weights[offset, k])[k * nfield : (k + 1) * nfield]
             target = targets[k : k + 1, :]
             row = target >> log2(ncols)
             key = ((row >> log2(half)) << log2(ncols)) + (target & (ncols - 1))
             group = row & (half - 1)
-            chosen = jnp.where(key_iota == key, 1.0, 0.0).astype(jnp.bfloat16)
+            keys.append(jnp.where(key_iota == key, 1.0, 0.0).astype(jnp.bfloat16))
             where_row = jnp.where(row_iota == group, 1.0, 0.0)
-            spread = (contrib[k][:, None, :] * where_row[None]).reshape(nfield * half, width)
-            top = spread.astype(jnp.bfloat16)
-            rest = (spread - top.astype(jnp.float32)).astype(jnp.bfloat16)
-            update = nt_dot(top, chosen) + nt_dot(rest, chosen)
-            if offset == 0 and k == 0:
-                acc[...] = update
-            else:
-                acc[...] += update
+            spread = (product[:, None, :] * where_row[None]).reshape(nfield * half, width)
+            tops.append(spread.astype(jnp.bfloat16))
+            rests.append((spread - tops[-1].astype(jnp.float32)).astype(jnp.bfloat16))
+        update = nt_dot(jnp.concatenate(tops + rests, 1), jnp.concatenate(keys + keys, 1))
+        if offset == 0:
+            acc[...] = update
+        else:
+            acc[...] += update
 
     first = (init_ref, edges_ref, rows_in, side_in)
     second = (flux.at[pl.ds(0, 3)], push_edges, push_rows_in, push_side_in)
     clear_halo(*first)
     clear_halo(*second)
-    weight_copy(0).wait()
-    deposit(0)
+    lax.fori_loop(0, nc, gather, 0)
 
     pl.semaphore_wait(barrier, total - 1)
     for offset in range(1, nc):
@@ -240,9 +239,10 @@
     send_halo(0, *first)
     send_fast(0, speed_ref)
 
-    for offset in range(1, nc):
+    for offset in range(nc):
         weight_copy(offset).wait()
-        block_copy(offset).wait_recv()
+        if offset:
+            block_copy(offset).wait_recv()
         deposit(offset)
 
     pushes = []
@@ -256,8 +256,6 @@
         if f == 2:
             push_edges[...] = pack_edges(pushes)
     send_halo(1, *second)
-    flux_copy = pltpu.make_async_copy(flux, flux_hbm, flux_sem)
-    flux_copy.start()
 
     high = nrows + 2 * HALO
     lane = lax.broadcasted_iota(jnp.int32, (high, ncols), 1)
@@ -324,7 +322,6 @@
     drain_halo(1, *second)
     for turn in range(NSUB):
         pltpu.make_async_copy(fastest.at[turn], fastest.at[turn], fast_send.at[turn]).wait()
-    flux_copy.wait()
 
 
 def shards(
@@ -333,30 +330,12 @@
     ocean_depth, wet_mask, sea_level, east_vel, north_vel,
 ):
     nfield, ncol = atm_fields.shape
-    ngroup, capacity, width = send_cols.shape[2:]
+    capacity, width = send_cols.shape[3:]
     nrows, ncols = ocean_depth.shape
     f32, bf16 = jnp.float32, jnp.bfloat16
     vmem = pl.BlockSpec(memory_space=pltpu.VMEM)
     smem = pl.BlockSpec(memory_space=pltpu.SMEM)
     anywhere = pl.BlockSpec(memory_space=pl.ANY)
-
-    blocks, targets, init, edges, speed = pl.pallas_call(
-        gather_kernel,
-        name="gather_columns",
-        out_shape=(
-            jax.ShapeDtypeStruct((ngroup, capacity * nfield, width), bf16),
-            jax.ShapeDtypeStruct((ngroup, capacity, width), jnp.int32),
-            jax.ShapeDtypeStruct((5, nrows, ncols), f32),
-            jax.ShapeDtypeStruct((nrows, ncols), f32),
-            jax.ShapeDtypeStruct((1, ncols), f32),
-        ),
-        in_specs=[vmem, vmem, smem] + [vmem] * 6,
-        out_specs=[vmem] * 5,
-        scratch_shapes=[pltpu.VMEM((nfield, ncol), f32)],
-    )(
-        atm_fields, send_cols[0, 0], live_blocks[0, 0], row_map[0, 0],
-        ocean_depth, wet_mask, sea_level, east_vel, north_vel,
-    )
 
     high = nrows + 2 * HALO
     dma = pltpu.SemaphoreType.DMA
@@ -364,17 +343,21 @@
         functools.partial(ocean_kernel, nc, nd),
         name="remap_and_step",
         out_shape=(
-            jax.ShapeDtypeStruct((nfield, nrows, ncols), f32),
-            jax.ShapeDtypeStruct((3, nrows, ncols), f32),
+            pltpu.VMEM((nfield, nrows, ncols), f32),
+            pltpu.VMEM((3, nrows, ncols), f32),
         ),
-        in_specs=[vmem] * 5 + [anywhere],
-        out_specs=[anywhere, vmem],
+        in_specs=[vmem, vmem, smem] + [vmem] * 6 + [anywhere],
+        out_specs=[vmem, vmem],
         scratch_shapes=[
+            pltpu.VMEM((nfield, ncol), f32),
+            pltpu.VMEM((nc, capacity * nfield, width), bf16),
+            pltpu.VMEM((nc, capacity, width), jnp.int32),
+            pltpu.VMEM((5, nrows, ncols), f32),
+            pltpu.VMEM((nrows, ncols), f32),
+            pltpu.VMEM((1, ncols), f32),
             pltpu.VMEM((nc, capacity, width, width), bf16),
             pltpu.VMEM((nc - 1, capacity * nfield, width), bf16),
-            pltpu.VMEM((capacity, nfield, width), f32),
             pltpu.VMEM((nfield * nrows // 2, 2 * ncols), f32),
-            pltpu.VMEM((nfield, nrows, ncols), f32),
             pltpu.VMEM((nrows, ncols), f32),
             pltpu.VMEM((2, 5, HALO, ncols), f32),
             pltpu.VMEM((2, high, ncols), f32),
@@ -383,7 +366,6 @@
             pltpu.VMEM((NSUB - 1, 1, ncols), f32),
             pltpu.VMEM((NSUB, nc * nd - 1, 1, ncols), f32),
             dma((nc,)),
-            dma(()),
             dma((nc - 1,)),
             dma((nc - 1,)),
             dma((2, 8)),
@@ -392,8 +374,22 @@
             dma((NSUB,)),
         ],
         compiler_params=pltpu.CompilerParams(collective_id=0, has_side_effects=True),
-    )(blocks, targets, init, edges, speed, remap_weights[0, 0])
-    return fluxes, state
+    )(
+        atm_fields, send_cols[0, 0], live_blocks[0, 0], row_map[0, 0],
+        ocean_depth, wet_mask, sea_level, east_vel, north_vel, remap_weights[0, 0],
+    )
+    return pl.pallas_call(
+        write_out,
+        name="write_out",
+        out_shape=(
+            jax.ShapeDtypeStruct(fluxes.shape, f32),
+            jax.ShapeDtypeStruct(state.shape, f32),
+        ),
+        in_specs=[vmem, vmem],
+        out_specs=[anywhere, anywhere],
+        scratch_shapes=[dma((2,))],
+        compiler_params=pltpu.CompilerParams(vmem_limit_bytes=4 << 20),
+    )(fluxes, state)
 
 
 def solution(mesh):

time: 40.6 us -> 34.1 us (0.84)
  local copies, waits for them, and re-layouts: 3.19 us -> 0 us
  Pallas kernels: 36.4 us -> 33.3 us
    unnamed x2 -> x0, local copies, waits for them, and re-layouts: 3.19 us -> none
    pallas_call x1, Pallas kernels: 2.93 us -> 0.77 us  [shards(): pl.pallas_call(write_out, name='write_out', out_shape=(jax.ShapeDtypeStru...]
    pallas_call x1, Pallas kernels: 33.5 us -> 32.5 us  [shards(): pl.pallas_call(functools.partial(ocean_kernel, nc, nd), name='remap_and_s...]
where the time goes in v2:
time: 34.1 us; the launch traced here: 33.9 us
  Pallas kernels  33.3 us (98%)
  between operations  0.64 us (2%)
    pallas_call x1, Pallas kernels, shards(): pl.pallas_call(functools.partial(ocean_kernel, nc, nd), name='remap_and_s...  32.5 us
    pallas_call x1, Pallas kernels, shards(): pl.pallas_call(write_out, name='write_out', out_shape=(jax.ShapeDtypeStru...  0.77 us

profile of v2, /device:TPU:0, one launch (start us, length us, event | category | flops | bytes accessed | tf_op | source)
XLA Modules:
  0.0 33.9 jit_solution(17769909706567695252)
XLA Ops:
  0.6 32.5 %remap_and_step.1 = (f32[24,32,128]{2,1,0:T(8,128)S(1)}, f32[3,32,128]{2,1,0:T(8,128)S(1)}) custom-call(bf16[24,2048]{1,0:T(8,128)(2,1)} %atm_ref.1, s32[4,4,256]{2,1,0:T(4,128)} %bitcast.5, s32[4]{0:T(128)} %bitcast.7, s32[4,4,256]{2,1,0:T(4,128)} %bitcast.6, f32[32,128]{1,0:T(8,128)} %depth_ref.1, s32[32,128]{1,0:T(8,128)} %wet_ref.1, ...), custom_call_target="tpu_custom_call" | custom-call | tf_op jit(solution)/shard_map/remap_and_step/pallas_call | solution.py:342
  33.2 0.8 %write_out.1 = (f32[24,32,128]{2,1,0:T(8,128)}, f32[3,32,128]{2,1,0:T(8,128)}) custom-call(f32[24,32,128]{2,1,0:T(8,128)S(1)} %get-tuple-element.4.flux_ref, f32[3,32,128]{2,1,0:T(8,128)S(1)} %get-tuple-element.5.state_ref), custom_call_target="tpu_custom_call" | custom-call | tf_op jit(solution)/shard_map/write_out/pallas_call | solution.py:381

commit v3 on v2

--- a/solution.py
+++ b/solution.py
@@ -69,7 +69,7 @@
         )
 
     def others(act):
-        for dc in range(nc):
+        for dc in reversed(range(nc)):
             c = lax.rem(me_c + dc, nc)
 
             def one(dd, carry, dc=dc, c=c):
@@ -77,7 +77,12 @@
                 act(dc * nd + dd - 1, (c, d))
                 return carry
 
-            lax.fori_loop(1 if dc == 0 else 0, nd, one, 0)
+            lower = 1 if dc == 0 else 0
+            if nd > 16:
+                lax.fori_loop(lower, nd, one, 0)
+                continue
+            for dd in sorted(range(lower, nd), key=lambda dd: min(dd, nd - dd)):
+                one(dd, 0)
 
     barrier = pltpu.get_barrier_semaphore()
     others(
@@ -205,6 +210,10 @@
     key_iota = lax.broadcasted_iota(jnp.int32, (2 * ncols, width), 0)
     row_iota = lax.broadcasted_iota(jnp.int32, (half, width), 0)
 
+    def spread(values, where_row):
+        tall = jnp.broadcast_to(values[:, None, :], (nfield, half, width)).astype(jnp.bfloat16)
+        return (tall * where_row[None]).reshape(nfield * half, width)
+
     def deposit(offset):
         source = lax.rem(me_c + nc - offset, nc)
         blocks = blocks_ref[0] if offset == 0 else arrived[offset - 1]
@@ -217,10 +226,10 @@
             key = ((row >> log2(half)) << log2(ncols)) + (target & (ncols - 1))
             group = row & (half - 1)
             keys.append(jnp.where(key_iota == key, 1.0, 0.0).astype(jnp.bfloat16))
-            where_row = jnp.where(row_iota == group, 1.0, 0.0)
-            spread = (product[:, None, :] * where_row[None]).reshape(nfield * half, width)
-            tops.append(spread.astype(jnp.bfloat16))
-            rests.append((spread - tops[-1].astype(jnp.float32)).astype(jnp.bfloat16))
+            where_row = jnp.where(row_iota == group, 1.0, 0.0).astype(jnp.bfloat16)
+            top = product.astype(jnp.bfloat16).astype(jnp.float32)
+            tops.append(spread(top, where_row))
+            rests.append(spread(product - top, where_row))
         update = nt_dot(jnp.concatenate(tops + rests, 1), jnp.concatenate(keys + keys, 1))
         if offset == 0:
             acc[...] = update
@@ -298,14 +307,16 @@
     for turn in range(NSUB):
         own = speed_ref if turn == 0 else fast.at[turn - 1]
         diverge = 0.5 * (across(conduct * east) + along(conduct * north))
+        still, rise = wet * level, wet * (fresh - diverge)
+        pull_x = rotation * north - 0.5 * across(still) + push_x - friction * east
+        pull_y = -rotation * east - 0.5 * along(still) + push_y - friction * north
+        slope_x, slope_y = 0.5 * across(rise), 0.5 * along(rise)
         wait_fast(turn)
         peak = jnp.maximum(jnp.max(fastest[turn], axis=0), own[...])
         step_dt = courant / jnp.max(peak, axis=1, keepdims=True)
-        level = wet * (level + step_dt * (fresh - diverge))
-        east, north = (
-            wet * (east + step_dt * (rotation * north - 0.5 * across(level) + push_x - friction * east)),
-            wet * (north + step_dt * (-rotation * east - 0.5 * along(level) + push_y - friction * north)),
-        )
+        level = still + step_dt * rise
+        east = wet * (east + step_dt * (pull_x - step_dt * slope_x))
+        north = wet * (north + step_dt * (pull_y - step_dt * slope_y))
         if turn < NSUB - 1:
             near_east = east[HALO : HALO + nrows, :ncols]
             near_north = north[HALO : HALO + nrows, :ncols]

time: 34.1 us -> 33 us (0.968)
  Pallas kernels: 33.3 us -> 32.2 us
    pallas_call x1, Pallas kernels: 32.5 us -> 31.4 us  [shards(): pl.pallas_call(functools.partial(ocean_kernel, nc, nd), name='remap_and_s...]
where the time goes in v3:
time: 33 us; the launch traced here: 32.8 us
  Pallas kernels  32.2 us (98%)
  between operations  0.64 us (2%)
    pallas_call x1, Pallas kernels, shards(): pl.pallas_call(functools.partial(ocean_kernel, nc, nd), name='remap_and_s...  31.4 us
    pallas_call x1, Pallas kernels, shards(): pl.pallas_call(write_out, name='write_out', out_shape=(jax.ShapeDtypeStru...  0.77 us

profile of v3, /device:TPU:0, one launch (start us, length us, event | category | flops | bytes accessed | tf_op | source)
XLA Modules:
  0.0 32.8 jit_solution(17081279759329094175)
XLA Ops:
  0.6 31.4 %remap_and_step.1 = (f32[24,32,128]{2,1,0:T(8,128)S(1)}, f32[3,32,128]{2,1,0:T(8,128)S(1)}) custom-call(bf16[24,2048]{1,0:T(8,128)(2,1)} %atm_ref.1, s32[4,4,256]{2,1,0:T(4,128)} %bitcast.5, s32[4]{0:T(128)} %bitcast.7, s32[4,4,256]{2,1,0:T(4,128)} %bitcast.6, f32[32,128]{1,0:T(8,128)} %depth_ref.1, s32[32,128]{1,0:T(8,128)} %wet_ref.1, ...), custom_call_target="tpu_custom_call" | custom-call | tf_op jit(solution)/shard_map/remap_and_step/pallas_call | solution.py:353
  32.1 0.8 %write_out.1 = (f32[24,32,128]{2,1,0:T(8,128)}, f32[3,32,128]{2,1,0:T(8,128)}) custom-call(f32[24,32,128]{2,1,0:T(8,128)S(1)} %get-tuple-element.4.flux_ref, f32[3,32,128]{2,1,0:T(8,128)S(1)} %get-tuple-element.5.state_ref), custom_call_target="tpu_custom_call" | custom-call | tf_op jit(solution)/shard_map/write_out/pallas_call | solution.py:392
